TPU v7x, 32 devices: a whole 2x2x4 slice. The times are simulated.
32 devices in a mesh: rows: 2 (over x), cols: 4 (over z), slabs: 2 (over y), trial: 2 (over core).
Axes of the slice: x: 2, y: 2, z: 4, core: 2. Of those that a mesh axis runs over, the one named last changes fastest.
Arguments:
- field_values: float32 [32, 64, 128, 128], P(('trial', 'rows'), 'cols', 'slabs'), parts along dimension 0, may hold values from 0.2 to 1.8
- crowding: float32 [32, 64, 128, 128], P(('trial', 'rows'), 'cols', 'slabs'), parts along dimension 0, may hold values from 0.5 to 2
Outputs:
- potential: float32 [32, 64, 128, 128], P(('trial', 'rows'), 'cols', 'slabs'), parts along dimension 0
- field_values_end: float32 [32, 64, 128, 128], P(('trial', 'rows'), 'cols', 'slabs'), parts along dimension 0
There are 2 independent parts, one for each index of `trial`. A program takes and returns all parts, laid end to end along the dimension named above; each array names one. Nothing has to cross between parts.
All inputs are finite; a program needn't handle non-finite values.
Results may differ from a plain program's by a relative error of at most 0.00002.
Values sent between devices are 32-bit elements; how exact they have to be, the bound alone decides.
A program may use at most 64 MiB of HBM per device.

v0:
```python
import functools

import jax
import jax.numpy as jnp
from jax import lax
from jax.experimental import pallas as pl
from jax.experimental.pallas import tpu as pltpu
from jax.sharding import PartitionSpec as P

STEPS = 3
MESH = pl.DeviceIdType.MESH
AXES = ("rows", "cols", "slabs")


def pieces_of(length, counts):
    for count in counts:
        if length % count == 0:
            return count
    return 1


def march_kernel(
    sizes, field, crowd, grid3, out_below,
    grid0, grid1, grid2, cells, y_in, y_out, total, below,
    x_send, x_recv, z_send, z_recv, y_send, y_recv, t_send, t_recv, load, face,
):
    J, I, K, L = field.shape
    grids = (grid0, grid1, grid2, grid3)
    Q = pieces_of(I, (2,))
    W = I // Q
    place = {axis: lax.axis_index(axis) for axis in AXES}
    has_target = {}
    has_source = {}
    for axis in AXES:
        later, earlier = place[axis] < sizes[axis] - 1, place[axis] > 0
        has_target[axis] = (later, earlier)
        has_source[axis] = (earlier, later)

    def target(axis, way):
        n = sizes[axis]
        return {axis: lax.rem(place[axis] + (1 if way == 0 else n - 1), n)}

    def face_load(way, q):
        plane = J - 1 if way == 0 else 0
        return pltpu.make_async_copy(
            field.at[plane, pl.ds(q * W, W)],
            grid0.at[1 + plane, pl.ds(1 + q * W, W)],
            face.at[way, q],
        )

    load_field = pltpu.make_async_copy(
        field.at[1 : J - 1], grid0.at[2:J, 1 : I + 1], load.at[0]
    )
    load_cells = pltpu.make_async_copy(crowd, cells, load.at[1])
    for q in range(Q):
        for way in (0, 1):
            face_load(way, q).start()

    barrier = pltpu.get_barrier_semaphore()
    for axis in AXES:
        if sizes[axis] > 1:
            for way in (0, 1):

                @pl.when(has_target[axis][way])
                def _():
                    pl.semaphore_signal(
                        barrier, inc=1, device_id=target(axis, way), device_id_type=MESH
                    )

    peers = jnp.int32(0)
    for axis in AXES:
        if sizes[axis] > 1:
            for way in (0, 1):
                peers = peers + has_source[axis][way].astype(jnp.int32)
    pl.semaphore_wait(barrier, peers)

    def x_copy(step, way, q):
        plane = J - 1 if way == 0 else 0
        halo = 0 if way == 0 else J + 1
        columns = pl.ds(1 + q * W, W)
        return pltpu.make_async_remote_copy(
            src_ref=grids[step].at[1 + plane, columns],
            dst_ref=grids[step].at[halo, columns],
            send_sem=x_send.at[step, way, q],
            recv_sem=x_recv.at[step, way, q],
            device_id=target("rows", way),
            device_id_type=MESH,
        )

    parts = ((0, 1), (1, J - 2), (J - 1, 1))

    def z_copy(step, way, part):
        first, count = parts[part]
        column = I - 1 if way == 0 else 0
        halo = 0 if way == 0 else I + 1
        if step == 0:
            source = field.at[pl.ds(first, count), column]
        else:
            source = grids[step].at[pl.ds(1 + first, count), 1 + column]
        return pltpu.make_async_remote_copy(
            src_ref=source,
            dst_ref=grids[step].at[pl.ds(1 + first, count), halo],
            send_sem=z_send.at[step, way, part],
            recv_sem=z_recv.at[step, way, part],
            device_id=target("cols", way),
            device_id_type=MESH,
        )

    def y_copy(step, way):
        return pltpu.make_async_remote_copy(
            src_ref=y_out.at[step, 1 - way],
            dst_ref=y_in.at[step, way],
            send_sem=y_send.at[step, way],
            recv_sem=y_recv.at[step, way],
            device_id=target("slabs", way),
            device_id_type=MESH,
        )

    def t_copy(q):
        columns = pl.ds(q * W, W)
        return pltpu.make_async_remote_copy(
            src_ref=total.at[columns],
            dst_ref=below.at[columns],
            send_sem=t_send.at[q],
            recv_sem=t_recv.at[q],
            device_id=target("rows", 0),
            device_id_type=MESH,
        )

    def start(axis, way, copies):
        if sizes[axis] > 1:

            @pl.when(has_target[axis][way])
            def _():
                for one in copies:
                    one.start()

    def sent(axis, way, copies):
        if sizes[axis] > 1:

            @pl.when(has_target[axis][way])
            def _():
                for one in copies:
                    one.wait_send()

    def arrived(axis, way, copies):
        if sizes[axis] > 1:

            @pl.when(has_source[axis][way])
            def _():
                for one in copies:
                    one.wait_recv()

    for q in range(Q):
        for way in (0, 1):
            face_load(way, q).wait()
            start("rows", way, [x_copy(0, way, q)])
    for way in (0, 1):
        start("cols", way, [z_copy(0, way, part) for part in range(3)])
    load_field.start()
    load_cells.start()

    zero = jnp.zeros((K, L), jnp.float32)
    for way in (0, 1):

        @pl.when(jnp.logical_not(has_source["rows"][way]))
        def _():
            def body(i, _):
                for step in range(STEPS):
                    grids[step][0 if way == 0 else J + 1, 1 + i] = zero
                if way == 0:
                    below[i] = zero
                return 0

            lax.fori_loop(0, I, body, 0)

        @pl.when(jnp.logical_not(has_source["cols"][way]))
        def _():
            def body(j, _):
                for step in range(STEPS):
                    grids[step][1 + j, 0 if way == 0 else I + 1] = zero
                return 0

            lax.fori_loop(0, J, body, 0)

        @pl.when(jnp.logical_not(has_source["slabs"][way]))
        def _():
            for step in range(STEPS):
                y_in[step, way] = jnp.zeros((J, I, L), jnp.float32)

    load_field.wait()

    def rims(step, j, i, value):
        y_out[step, 0, j, pl.ds(i, 1), :] = value[0:1]
        y_out[step, 1, j, pl.ds(i, 1), :] = value[K - 1 : K]

    def first_rims(j, _):
        def body(i, _):
            for side, row in ((0, 0), (1, K - 1)):
                y_out[0, side, j, pl.ds(i, 1), :] = grid0[1 + j, 1 + i, pl.ds(row, 1), :]
            return 0

        return lax.fori_loop(0, I, body, 0)

    lax.fori_loop(0, J, first_rims, 0)
    for way in (0, 1):
        start("slabs", way, [y_copy(0, way)])
    load_cells.wait()

    def tile(step, j, i):
        old, new = grids[step - 1], grids[step]
        middle = old[1 + j, 1 + i]
        before = y_in[step - 1, 0, j, pl.ds(i, 1), :]
        after = y_in[step - 1, 1, j, pl.ds(i, 1), :]
        near = jnp.concatenate([before, middle[: K - 1]], axis=0)
        far = jnp.concatenate([middle[1:], after], axis=0)
        around = (
            (old[j, 1 + i] + old[2 + j, 1 + i])
            + (old[1 + j, i] + old[1 + j, 2 + i])
            + (near + far)
        )
        value = middle * (0.6 - 0.2 * (middle * cells[j, i])) + 0.1 * around
        if step < STEPS:
            new[1 + j, 1 + i] = value
            rims(step, j, i, value)
        else:
            new[j, i] = value

    for step in range(1, STEPS + 1):
        last = step == STEPS
        for way in (0, 1):
            arrived("slabs", way, [y_copy(step - 1, way)])

        def inner(j, _):
            def body(i, _):
                tile(step, j, i)
                return 0

            return lax.fori_loop(1, I - 1, body, 0)

        lax.fori_loop(1, J - 1, inner, 0)
        for way in (0, 1):
            arrived("cols", way, [z_copy(step - 1, way, part) for part in range(3)])

        def edges(j, _):
            tile(step, j, 0)
            tile(step, j, I - 1)
            return 0

        lax.fori_loop(1, J - 1, edges, 0)
        if not last:
            for way in (0, 1):
                start("cols", way, [z_copy(step, way, 1)])
        for q in range(Q):
            for way in (0, 1):
                arrived("rows", way, [x_copy(step - 1, way, q)])

            def faces(i, _):
                tile(step, 0, i)
                tile(step, J - 1, i)
                return 0

            lax.fori_loop(q * W, (q + 1) * W, faces, 0)
            if not last:
                for way in (0, 1):
                    start("rows", way, [x_copy(step, way, q)])
            else:

                @pl.when(has_target["rows"][0])
                def _():
                    def add(i, _):
                        value = grid3[0, i]
                        for j in range(1, J):
                            value = value + grid3[j, i]
                        total[i] = value
                        return 0

                    lax.fori_loop(q * W, (q + 1) * W, add, 0)

                @pl.when(jnp.logical_not(has_source["rows"][0]))
                def _():
                    start("rows", 0, [t_copy(q)])
        if not last:
            for way in (0, 1):
                start("cols", way, [z_copy(step, way, 0), z_copy(step, way, 2)])
                start("slabs", way, [y_copy(step, way)])

    for q in range(Q):

        @pl.when(has_source["rows"][0])
        def _():
            if sizes["rows"] > 1:
                t_copy(q).wait_recv()

                @pl.when(has_target["rows"][0])
                def _():
                    def add(i, _):
                        total[i] = total[i] + below[i]
                        return 0

                    lax.fori_loop(q * W, (q + 1) * W, add, 0)
                    t_copy(q).start()

        columns = pl.ds(q * W, W)
        out_below[columns] = below[columns]

    for step in range(STEPS):
        for way in (0, 1):
            sent("rows", way, [x_copy(step, way, q) for q in range(Q)])
            sent("cols", way, [z_copy(step, way, part) for part in range(3)])
            sent("slabs", way, [y_copy(step, way)])
    sent("rows", 0, [t_copy(q) for q in range(Q)])

def sum_kernel(scale, field, below, potential, field_end, sums, end_sem, sum_sem):
    J, I = field.shape[0], field.shape[1]
    Q = pieces_of(I, (4, 2))
    W = I // Q

    whole = pltpu.make_async_copy(field, field_end, end_sem)
    whole.start()

    def piece(q):
        columns = pl.ds(q * W, W)
        return pltpu.make_async_copy(
            sums.at[:, columns], potential.at[:, columns], sum_sem.at[q]
        )

    for q in range(Q):

        def body(i, _):
            value = below[i]
            for j in range(J):
                value = value + field[j, i]
                sums[j, i] = value * scale
            return 0

        lax.fori_loop(q * W, (q + 1) * W, body, 0)
        piece(q).start()
    for q in range(Q):
        piece(q).wait()
    whole.wait()


def solution(mesh):
    sizes = {axis: mesh.shape[axis] for axis in AXES}

    def on_device(field_values, crowding):
        J, I, K, L = field_values.shape
        Q = pieces_of(I, (2,))
        padded = pltpu.VMEM((J + 2, I + 2, K, L), jnp.float32)
        block = jax.ShapeDtypeStruct((J, I, K, L), jnp.float32)
        vector = pl.BlockSpec(memory_space=pltpu.VMEM)
        anywhere = pl.BlockSpec(memory_space=pl.ANY)
        dma = pltpu.SemaphoreType.DMA
        field_end, below = pl.pallas_call(
            functools.partial(march_kernel, sizes),
            out_shape=(
                pltpu.VMEM((J, I, K, L), jnp.float32),
                pltpu.VMEM((I, K, L), jnp.float32),
            ),
            in_specs=[anywhere] * 2,
            out_specs=(vector, vector),
            scratch_shapes=[
                padded,
                padded,
                padded,
                pltpu.VMEM((J, I, K, L), jnp.float32),
                pltpu.VMEM((STEPS, 2, J, I, L), jnp.float32),
                pltpu.VMEM((STEPS, 2, J, I, L), jnp.float32),
                pltpu.VMEM((I, K, L), jnp.float32),
                pltpu.VMEM((I, K, L), jnp.float32),
                dma((STEPS, 2, Q)),
                dma((STEPS, 2, Q)),
                dma((STEPS, 2, 3)),
                dma((STEPS, 2, 3)),
                dma((STEPS, 2)),
                dma((STEPS, 2)),
                dma((Q,)),
                dma((Q,)),
                dma((2,)),
                dma((2, Q)),
            ],
            compiler_params=pltpu.CompilerParams(
                collective_id=0,
                has_side_effects=True,
                vmem_limit_bytes=57 * 1024 * 1024,
            ),
        )(field_values, crowding)

        potential, field_end = pl.pallas_call(
            functools.partial(sum_kernel, 1.0 / (J * sizes["rows"])),
            out_shape=(block, block),
            in_specs=[vector, vector],
            out_specs=(anywhere, anywhere),
            scratch_shapes=[pltpu.VMEM((J, I, K, L), jnp.float32), dma, dma((pieces_of(I, (4, 2)),))],
            compiler_params=pltpu.CompilerParams(vmem_limit_bytes=16 * 1024 * 1024),
        )(field_end, below)
        return potential, field_end

    spec = P(("trial", "rows"), "cols", "slabs", None)
    return jax.shard_map(
        on_device,
        mesh=mesh,
        in_specs=(spec, spec),
        out_specs=(spec, spec),
        check_vma=False,
    )
```

profile of v0, /device:TPU:0, one launch (start us, length us, event | category | flops | bytes accessed | tf_op | source)
XLA Modules:
  0.0 52.7 jit_solution(2337793874574652345)
XLA Ops:
  0.6 48.8 %shard_map.41 = (f32[8,16,64,128]{3,2,1,0:T(8,128)S(1)}, f32[16,64,128]{2,1,0:T(8,128)S(1)}) custom-call(f32[8,16,64,128]{3,2,1,0:T(8,128)} %field.1, f32[8,16,64,128]{3,2,1,0:T(8,128)} %crowd.1), custom_call_target="tpu_custom_call" | custom-call | tf_op jit(solution)/shard_map/pallas_call | solution.py:355
  49.4 3.3 %shard_map.42 = (f32[8,16,64,128]{3,2,1,0:T(8,128)}, f32[8,16,64,128]{3,2,1,0:T(8,128)}) custom-call(f32[8,16,64,128]{3,2,1,0:T(8,128)S(1)} %get-tuple-element.4.field, f32[16,64,128]{2,1,0:T(8,128)S(1)} %get-tuple-element.5.below), custom_call_target="tpu_custom_call" | custom-call | tf_op jit(solution)/shard_map/pallas_call | solution.py:390
where the time goes:
time: 52.9 us; the launch traced here: 52.7 us
  Pallas kernels  52.1 us (98%)
  between operations  0.64 us (1%)
    pallas_call x1, Pallas kernels, on_device(): pl.pallas_call(functools.partial(march_kernel, sizes), out_shape=(pltpu.V...  48.8 us
    pallas_call x1, Pallas kernels, on_device(): pl.pallas_call(functools.partial(sum_kernel, 1.0 / (J * sizes['rows'])),...  3.34 us

commit v1 on v0

v1 whole, which is shorter than its diff:
```python
import functools

import jax
import jax.numpy as jnp
from jax import lax
from jax.experimental import pallas as pl
from jax.experimental.pallas import tpu as pltpu
from jax.sharding import PartitionSpec as P

STEPS = 3
MESH = pl.DeviceIdType.MESH
AXES = ("rows", "cols", "slabs")
PAD = 8


def pieces_of(length, counts):
    for count in counts:
        if length % count == 0:
            return count
    return 1


def segments_of(I):
    if I % 4:
        return ((0, I),)
    return ((0, I // 2), (I // 2, I // 4), (I - I // 4, I // 4))


def cut(I, eighths):
    lead = I * eighths // 8 if I % 8 == 0 else I - I // 2
    return ((0, lead), (lead, I - lead))


def loop(low, high, body):
    def step(at, _):
        body(at)
        return 0

    lax.fori_loop(low, high, step, 0)


def march_kernel(sizes, field, crowd, final, *refs):
    segments = segments_of(field.shape[1])
    totals, refs = refs[: len(segments)], refs[len(segments) :]
    (
        grid0, grid1, grid2, cells, x_in, part, y_in, y_out,
        x_send, x_recv, z_send, z_recv, y_send, y_recv, load, go,
    ) = refs
    J, I, K, L = field.shape
    grids = (grid0, grid1, grid2)
    x_parts = [((0, I),)] * (STEPS - 2) + [cut(I, 6), cut(I, 6)]
    x_slot = [step + max(step - STEPS + 2, 0) for step in range(STEPS)]
    U = pieces_of(I, (4, 2))
    inside = pl.ds(PAD, K)
    place = {axis: lax.axis_index(axis) for axis in AXES}
    has_target = {}
    has_source = {}
    for axis in AXES:
        later, earlier = place[axis] < sizes[axis] - 1, place[axis] > 0
        has_target[axis] = (later, earlier)
        has_source[axis] = (earlier, later)
    trial = lax.axis_index("trial")
    first = lax.rem(trial, 2) == 0
    paired = sizes["trial"] % 2 == 0 and sizes["rows"] > 1
    partner = {"trial": trial + 1 - 2 * lax.rem(trial, 2)}
    out_plane = (J - 1, 0)
    in_plane = (0, J - 1)
    out_at = (0, 1)
    in_at = (1, 0)
    rows = ((0, 2), (2, J - 2))

    def target(axis, way):
        n = sizes[axis]
        return {axis: lax.rem(place[axis] + (1 if way == 0 else n - 1), n)}

    load_field = [
        pltpu.make_async_copy(
            field.at[: J - 1], grid0.at[1:J, 1 : I + 1, inside], load.at[0]
        ),
        pltpu.make_async_copy(
            field.at[J - 1], grid0.at[0, 1 : I + 1, inside], load.at[1]
        ),
    ]
    load_cells = pltpu.make_async_copy(crowd, cells, load.at[2])
    for one in load_field:
        one.start()
    load_cells.start()

    barrier = pltpu.get_barrier_semaphore()
    peers = jnp.int32(1 if paired else 0)
    for axis in AXES:
        if sizes[axis] > 1:
            for way in (0, 1):

                @pl.when(has_target[axis][way])
                def _():
                    pl.semaphore_signal(
                        barrier, inc=1, device_id=target(axis, way), device_id_type=MESH
                    )

                peers = peers + has_source[axis][way].astype(jnp.int32)
    if paired:
        pl.semaphore_signal(barrier, inc=1, device_id=partner, device_id_type=MESH)
    pl.semaphore_wait(barrier, peers)

    def x_copy(step, way, n):
        at, count = x_parts[step][n]
        columns = pl.ds(at, count)
        if step == 0:
            source = field.at[out_plane[way], columns]
        else:
            source = part.at[step - 1, way, columns]
        return pltpu.make_async_remote_copy(
            src_ref=source,
            dst_ref=x_in.at[step, way, columns],
            send_sem=x_send.at[x_slot[step] + n, way],
            recv_sem=x_recv.at[x_slot[step] + n, way],
            device_id=target("rows", way),
            device_id_type=MESH,
        )

    def z_copy(step, way, piece):
        column = I - 1 if way == 0 else 0
        halo = 0 if way == 0 else I + 1
        if step == 0:
            at, count = ((0, 1), (1, J - 1))[piece]
            source = field.at[pl.ds((J - 1, 0)[piece], count), column]
        else:
            at, count = rows[piece]
            source = grids[step].at[pl.ds(at, count), 1 + column, inside]
        return pltpu.make_async_remote_copy(
            src_ref=source,
            dst_ref=grids[step].at[pl.ds(at, count), halo, inside],
            send_sem=z_send.at[way, piece],
            recv_sem=z_recv.at[step, way, piece],
            device_id=target("cols", way),
            device_id_type=MESH,
        )

    def y_copy(step, way, piece):
        at, count = rows[piece]
        return pltpu.make_async_remote_copy(
            src_ref=y_out.at[step, 1 - way, pl.ds(at, count)],
            dst_ref=y_in.at[step, way, pl.ds(at, count)],
            send_sem=y_send.at[way, piece],
            recv_sem=y_recv.at[step, way, piece],
            device_id=target("slabs", way),
            device_id_type=MESH,
        )

    def start(axis, way, copies):
        if sizes[axis] > 1:

            @pl.when(has_target[axis][way])
            def _():
                for one in copies:
                    one.start()

    def sent(axis, way, copies):
        if sizes[axis] > 1:

            @pl.when(has_target[axis][way])
            def _():
                for one in copies:
                    one.wait_send()

    def arrived(axis, way, copies):
        if sizes[axis] > 1:

            @pl.when(has_source[axis][way])
            def _():
                for one in copies:
                    one.wait_recv()

    def send_rims(step, pieces):
        for way in (0, 1):
            if step > 0:
                sent("slabs", way, [y_copy(step - 1, way, piece) for piece in pieces])
            start("slabs", way, [y_copy(step, way, piece) for piece in pieces])

    def send_columns(step, pieces):
        for way in (0, 1):
            if step > 0:
                sent("cols", way, [z_copy(step - 1, way, piece) for piece in pieces])
            start("cols", way, [z_copy(step, way, piece) for piece in pieces])

    def receive(step, pieces):
        grid = grids[step]
        for way in (0, 1):
            arrived("slabs", way, [y_copy(step, way, piece) for piece in pieces])
            row = PAD - 1 if way == 0 else PAD + K

            def place_row(j):
                def body(i):
                    for u in range(U):
                        at = i * U + u
                        grid[j, 1 + at, pl.ds(row, 1), :] = y_in[
                            step, way, j, pl.ds(at, 1), :
                        ]

                loop(0, I // U, body)

            @pl.when(has_source["slabs"][way])
            def _():
                for piece in pieces:
                    at, count = rows[piece]
                    loop(at, at + count, place_row)

        for way in (0, 1):
            arrived("cols", way, [z_copy(step, way, piece) for piece in pieces])

    def keep_rims(step, j):
        def body(i):
            for u in range(U):
                at = i * U + u
                for side, row in ((0, PAD), (1, PAD + K - 1)):
                    y_out[step, side, j, pl.ds(at, 1), :] = grids[step][
                        j, 1 + at, pl.ds(row, 1), :
                    ]

        loop(0, I // U, body)

    def tile(step, j, at, i, beside):
        old = grids[step - 1]
        middle = old[at, 1 + i, inside]
        around = (old[at, i, inside] + old[at, 2 + i, inside]) + (
            old[at, 1 + i, pl.ds(PAD - 1, K)] + old[at, 1 + i, pl.ds(PAD + 1, K)]
        )
        for other in beside:
            around = around + old[other, 1 + i, inside]
        return middle * (0.6 - 0.2 * (middle * cells[j, i])) + 0.1 * around

    def interior(step, low, high):
        def row(j):
            def body(i):
                for u in range(U):
                    at = i * U + u
                    value = tile(step, j, j + 1, at, (j, lax.rem(j + 2, J)))
                    if step < STEPS:
                        grids[step][j + 1, 1 + at, inside] = value
                        y_out[step, 0, j + 1, pl.ds(at, 1), :] = value[0:1]
                        y_out[step, 1, j + 1, pl.ds(at, 1), :] = value[K - 1 : K]
                    else:
                        final[j, at] = value

            loop(0, I // U, body)

        loop(low, high, row)

    def faces(step):
        V = pieces_of(I, (2,))

        def body(i):
            for v in range(V):
                at = i * V + v
                for way in (0, 1):
                    kept = out_at[way]
                    value = tile(step, out_plane[way], kept, at, ((J - 1, 2)[way],))
                    if step < STEPS:
                        grids[step][kept, 1 + at, inside] = value
                        part[step - 1, way, at] = value
                    else:
                        final[out_plane[way], at] = value

        loop(0, I // V, body)

    def halo(step, way, at):
        value = x_in[step, way, at]
        if step > 0:
            value = value + 0.1 * grids[step - 1][in_at[way], 1 + at, inside]
        return 0.1 * value

    def finish(step):
        def columns(way, low, high, n):
            V = pieces_of(high - low, (2,))

            def body(i):
                for v in range(V):
                    at = low + i * V + v
                    extra = halo(step - 1, way, at)
                    if step < STEPS:
                        grids[step][in_at[way], 1 + at, inside] = (
                            part[step - 1, 1 - way, at] + extra
                        )
                    else:
                        plane, here = in_plane[way], at - segments[n][0]
                        final[plane, at] = final[plane, at] + extra
                        totals[n][here] = totals[n][here] + extra

            loop(0, (high - low) // V, body)

        for part_n, (begin, count) in enumerate(x_parts[step - 1]):
            for way in (0, 1):
                arrived("rows", way, [x_copy(step - 1, way, part_n)])

                @pl.when(has_source["rows"][way])
                def _():
                    if step < STEPS:
                        columns(way, begin, begin + count, 0)
                        return
                    for n, (at, width) in enumerate(segments):
                        low, high = max(at, begin), min(at + width, begin + count)
                        if low < high:
                            columns(way, low, high, n)

    def send_plane(step, low=0, high=2):
        for way in (0, 1):
            count = len(x_parts[step])
            start("rows", way, [x_copy(step, way, n) for n in range(count)[low:high]])

    send_plane(0)
    send_columns(0, (0, 1))

    zero = jnp.zeros((K, L), jnp.float32)
    for way in (0, 1):

        @pl.when(jnp.logical_not(has_source["slabs"][way]))
        def _():
            row = PAD - 1 if way == 0 else PAD + K

            def body(j):
                for step in range(STEPS):
                    for i in range(I):
                        grids[step][j, 1 + i, pl.ds(row, 1), :] = zero[0:1]

            loop(0, J, body)

        @pl.when(jnp.logical_not(has_source["cols"][way]))
        def _():
            def body(j):
                for step in range(STEPS):
                    grids[step][j, 0 if way == 0 else I + 1, inside] = zero

            loop(0, J, body)

    for one in load_field:
        one.wait()
    loop(0, J, functools.partial(keep_rims, 0))
    send_rims(0, (0, 1))
    load_cells.wait()

    for step in range(1, STEPS + 1):
        last = step == STEPS
        if step > 1:
            receive(step - 1, (1,))
            if last and paired:
                interior(step, 1, J // 2)

                @pl.when(first)
                def _():
                    for way in (0, 1):
                        sent("rows", way, [x_copy(step - 1, way, 0)])
                    pl.semaphore_signal(go, inc=1, device_id=partner, device_id_type=MESH)

                interior(step, J // 2, J - 1)
            else:
                interior(step, 1, J - 1)
            if not last:
                send_rims(step, (1,))
                send_columns(step, (1,))
        receive(step - 1, (0, 1) if step == 1 else (0,))
        faces(step)
        if step == STEPS - 1 and paired:

            @pl.when(first)
            def _():
                send_plane(step)

            @pl.when(jnp.logical_not(first))
            def _():
                pl.semaphore_wait(go, 1)
                send_plane(step - 1, 1, 2)
                send_plane(step)

        elif step == STEPS - 2 and paired:
            send_plane(step, 0, 1)

            @pl.when(first)
            def _():
                send_plane(step, 1, 2)

        elif not last:
            send_plane(step)
        if step == 1:
            interior(1, 1, J - 1)
            send_rims(1, (1,))
            send_columns(1, (1,))
        if last:
            for n, (first_at, count) in enumerate(segments):

                def add(here):
                    value = final[0, first_at + here]
                    for j in range(1, J):
                        value = value + final[j, first_at + here]
                    totals[n][here] = value

                loop(0, count, add)
        finish(step)
        if not last:
            loop(0, 2, functools.partial(keep_rims, step))
            send_rims(step, (0,))
            send_columns(step, (0,))

    for step in range(STEPS):
        for way in (0, 1):
            plane = [x_copy(step, way, n) for n in range(len(x_parts[step]))]
            if step == STEPS - 1 and paired:

                @pl.when(first)
                def _():
                    sent("rows", way, plane[1:])

                @pl.when(jnp.logical_not(first))
                def _():
                    sent("rows", way, plane)

            else:
                sent("rows", way, plane)
    for way in (0, 1):
        sent("cols", way, [z_copy(STEPS - 1, way, piece) for piece in (0, 1)])
        sent("slabs", way, [y_copy(STEPS - 1, way, piece) for piece in (0, 1)])


def end_kernel(scale, final, field_end, potential, sums, end_sem, sum_sem):
    J, I = final.shape[0], final.shape[1]
    pieces = sum_sem.shape[0]
    W = I // pieces
    whole = pltpu.make_async_copy(final, field_end, end_sem)
    whole.start()

    def piece(q):
        columns = pl.ds(q * W, W)
        return pltpu.make_async_copy(
            sums.at[:, columns], potential.at[:, columns], sum_sem.at[q]
        )

    @pl.when(lax.axis_index("rows") == 0)
    def _():
        for q in range(pieces):

            def body(i):
                value = final[0, i]
                sums[0, i] = value * scale
                for j in range(1, J):
                    value = value + final[j, i]
                    sums[j, i] = value * scale

            loop(q * W, (q + 1) * W, body)
            piece(q).start()
        for q in range(pieces):
            piece(q).wait()

    whole.wait()


def sum_kernel(scale, at, final, below, _, potential, sums, sem):
    J = final.shape[0]
    W = below.shape[0]

    def piece(i):
        return pltpu.make_async_copy(
            sums.at[:, i], potential.at[:, at + i], sem.at[i]
        )

    @pl.when(lax.axis_index("rows") > 0)
    def _():
        for i in range(W):
            value = below[i]
            for j in range(J):
                value = value + final[j, at + i]
                sums[j, i] = value * scale
            piece(i).start()
        for i in range(W):
            piece(i).wait()


def totals_below(total, n):
    below = lax.ppermute(total, "rows", [(r, r + 1) for r in range(n - 1)])
    reach = 1
    while reach < n - 1:
        below = below + lax.ppermute(
            below, "rows", [(r, r + reach) for r in range(n - reach)]
        )
        reach *= 2
    return below


def solution(mesh):
    sizes = {axis: mesh.shape[axis] for axis in AXES + ("trial",)}

    def on_device(field_values, crowding):
        J, I, K, L = field_values.shape
        widths = [width for _, width in segments_of(I)]
        N = len(widths)
        padded = pltpu.VMEM((J, I + 2, K + 2 * PAD, L), jnp.float32)
        block = jax.ShapeDtypeStruct((J, I, K, L), jnp.float32)
        vector = pl.BlockSpec(memory_space=pltpu.VMEM)
        anywhere = pl.BlockSpec(memory_space=pl.ANY)
        dma = pltpu.SemaphoreType.DMA
        final, *totals = pl.pallas_call(
            functools.partial(march_kernel, sizes),
            out_shape=(pltpu.VMEM((J, I, K, L), jnp.float32),)
            + tuple(pltpu.VMEM((width, K, L), jnp.float32) for width in widths),
            in_specs=[anywhere] * 2,
            out_specs=(vector,) * (1 + N),
            scratch_shapes=[
                padded,
                padded,
                padded,
                pltpu.VMEM((J, I, K, L), jnp.float32),
                pltpu.VMEM((STEPS, 2, I, K, L), jnp.float32),
                pltpu.VMEM((STEPS - 1, 2, I, K, L), jnp.float32),
                pltpu.VMEM((STEPS, 2, J, I, L), jnp.float32),
                pltpu.VMEM((STEPS, 2, J, I, L), jnp.float32),
                dma((STEPS + 2, 2)),
                dma((STEPS + 2, 2)),
                dma((2, 2)),
                dma((STEPS, 2, 2)),
                dma((2, 2)),
                dma((STEPS, 2, 2)),
                dma((3,)),
                pltpu.SemaphoreType.REGULAR,
            ],
            compiler_params=pltpu.CompilerParams(
                collective_id=0,
                has_side_effects=True,
                vmem_limit_bytes=50 * 1024 * 1024,
            ),
        )(field_values, crowding)

        bytes_out = J * I * K * L * 4
        scale = 1.0 / (J * sizes["rows"])
        pieces = pieces_of(I, (4, 2))
        belows = []
        if sizes["rows"] > 1:
            belows = [totals_below(total, sizes["rows"]) for total in totals]
        field_end, potential = pl.pallas_call(
            functools.partial(end_kernel, scale),
            out_shape=(block, block),
            in_specs=[vector],
            out_specs=(anywhere, anywhere),
            scratch_shapes=[pltpu.VMEM((J, I, K, L), jnp.float32), dma, dma((pieces,))],
            compiler_params=pltpu.CompilerParams(vmem_limit_bytes=5 * 1024 * 1024),
            cost_estimate=pl.CostEstimate(
                flops=4 * bytes_out, bytes_accessed=bytes_out, transcendentals=0
            ),
        )(final)
        for (at, width), below in zip(segments_of(I), belows):
            potential = pl.pallas_call(
                functools.partial(sum_kernel, scale, at),
                out_shape=block,
                in_specs=[vector, vector, anywhere],
                out_specs=anywhere,
                scratch_shapes=[
                    pltpu.VMEM((J, width, K, L), jnp.float32),
                    dma((width,)),
                ],
                input_output_aliases={2: 0},
                compiler_params=pltpu.CompilerParams(vmem_limit_bytes=5 * 1024 * 1024),
                cost_estimate=pl.CostEstimate(
                    flops=bytes_out,
                    bytes_accessed=bytes_out * width // I,
                    transcendentals=0,
                ),
            )(final, below, potential)
        return potential, field_end

    spec = P(("trial", "rows"), "cols", "slabs", None)
    return jax.shard_map(
        on_device,
        mesh=mesh,
        in_specs=(spec, spec),
        out_specs=(spec, spec),
        check_vma=False,
    )
```

time: 52.9 us -> 49.6 us (0.938)
  the two profiles are of different devices: /device:TPU:0 before, /device:TPU:3 now
where the time goes in v1:
time: 49.6 us; the launch traced here: 49.4 us
  Pallas kernels  43.4 us (88%)
  starting transfers between devices  3.88 us (8%)
  waiting for transfers between devices  1.51 us (3%)
  between operations  0.69 us (1%)
    pallas_call x1, Pallas kernels, on_device(): pl.pallas_call(functools.partial(march_kernel, sizes), out_shape=(pltpu.V...  37.9 us
    ppermute x3, starting transfers between devices, totals_below(): below = lax.ppermute(total, 'rows', [(r, r + 1) for r in range(n - 1)])  3.88 us
    pallas_call x3, Pallas kernels, on_device(): pl.pallas_call(functools.partial(sum_kernel, scale, at), out_shape=block,...  3.44 us
    pallas_call x1, Pallas kernels, on_device(): pl.pallas_call(functools.partial(end_kernel, scale), out_shape=(block, bl...  2.06 us
    ppermute x3, waiting for transfers between devices, totals_below(): below = lax.ppermute(total, 'rows', [(r, r + 1) for r in range(n - 1)])  1.51 us
  transfers between devices with their start and end apart: 3, of which 2 were waited for; matrix products, arithmetic and copies ran while one was open for 0% of the time, Pallas kernels for 9%

profile of v1, /device:TPU:3, one launch (start us, length us, event | category | flops | bytes accessed | tf_op | source)
XLA Modules:
  0.0 49.4 jit_solution(10751038789373559113)
XLA Ops:
  0.6 37.9 %shard_map.41 = (f32[8,16,64,128]{3,2,1,0:T(8,128)S(1)}, f32[8,64,128]{2,1,0:T(8,128)S(1)}, f32[4,64,128]{2,1,0:T(8,128)S(1)}, f32[4,64,128]{2,1,0:T(8,128)S(1)}) custom-call(f32[8,16,64,128]{3,2,1,0:T(8,128)} %field.1, f32[8,16,64,128]{3,2,1,0:T(8,128)} %crowd.1), custom_call_target="tpu_custom_call" | custom-call | tf_op jit(solution)/shard_map/pallas_call | solution.py:500
  38.5 1.3 %collective-permute-start.2 = (f32[8,64,128]{2,1,0:T(8,128)S(1)}, f32[8,64,128]{2,1,0:T(8,128)S(1)}, u32[]{:S(2)}, u32[]{:S(2)}) collective-permute-start(f32[8,64,128]{2,1,0:T(8,128)S(1)} %get-tuple-element.11), channel_id=1, source_target_pairs={{0,16},{1,17},{2,18},{3,19},{4,20},{5,21},{6,22},{7,23},{8,24},{9,... | collective-permute-start | bytes 786440 | tf_op jit(solution)/shard_map/ppermute | solution.py:478
  39.8 1.3 %collective-permute-start.1 = (f32[4,64,128]{2,1,0:T(8,128)S(1)}, f32[4,64,128]{2,1,0:T(8,128)S(1)}, u32[]{:S(2)}, u32[]{:S(2)}) collective-permute-start(f32[4,64,128]{2,1,0:T(8,128)S(1)} %get-tuple-element.10), channel_id=1, source_target_pairs={{0,16},{1,17},{2,18},{3,19},{4,20},{5,21},{6,22},{7,23},{8,24},{9,... | collective-permute-start | bytes 393224 | tf_op jit(solution)/shard_map/ppermute | solution.py:478
  41.1 1.3 %collective-permute-start = (f32[4,64,128]{2,1,0:T(8,128)S(1)}, f32[4,64,128]{2,1,0:T(8,128)S(1)}, u32[]{:S(2)}, u32[]{:S(2)}) collective-permute-start(f32[4,64,128]{2,1,0:T(8,128)S(1)} %get-tuple-element.9), channel_id=1, source_target_pairs={{0,16},{1,17},{2,18},{3,19},{4,20},{5,21},{6,22},{7,23},{8,24},{9,... | collective-permute-start | bytes 393224 | tf_op jit(solution)/shard_map/ppermute | solution.py:478
  42.4 2.1 %shard_map.42 = (f32[8,16,64,128]{3,2,1,0:T(8,128)}, f32[8,16,64,128]{3,2,1,0:T(8,128)}) custom-call(f32[8,16,64,128]{3,2,1,0:T(8,128)S(1)} %get-tuple-element.8.final), custom_call_target="tpu_custom_call" | custom-call | flops 16777216 | bytes 4194304 | tf_op jit(solution)/shard_map/pallas_call | solution.py:537
  44.5 1.1 %collective-permute-done.2.below = f32[8,64,128]{2,1,0:T(8,128)S(1)} collective-permute-done((f32[8,64,128]{2,1,0:T(8,128)S(1)}, f32[8,64,128]{2,1,0:T(8,128)S(1)}, u32[]{:S(2)}, u32[]{:S(2)}) %collective-permute-start.2) | collective-permute-done | bytes 262176 | tf_op jit(solution)/shard_map/ppermute | solution.py:478
  45.6 1.4 %shard_map.43._ = f32[8,16,64,128]{3,2,1,0:T(8,128)} custom-call(f32[8,16,64,128]{3,2,1,0:T(8,128)S(1)} %get-tuple-element.8.final, f32[8,64,128]{2,1,0:T(8,128)S(1)} %collective-permute-done.2.below, f32[8,16,64,128]{3,2,1,0:T(8,128)} %get-tuple-element.12._), custom_call_target="tpu_custom_call", output_to_operand_aliasing={{}: (2, {})} | custom-call | flops 4194304 | bytes 2097152 | tf_op jit(solution)/shard_map/pallas_call | solution.py:549
  47.0 0.0 collective-permute-done.1.below
  47.0 1.0 %shard_map.44._ = f32[8,16,64,128]{3,2,1,0:T(8,128)} custom-call(f32[8,16,64,128]{3,2,1,0:T(8,128)S(1)} %get-tuple-element.8.final, f32[4,64,128]{2,1,0:T(8,128)S(1)} %collective-permute-done.1.below, f32[8,16,64,128]{3,2,1,0:T(8,128)} %shard_map.43._), custom_call_target="tpu_custom_call", output_to_operand_aliasing={{}: (2, {})} | custom-call | flops 4194304 | bytes 1048576 | tf_op jit(solution)/shard_map/pallas_call | solution.py:549
  48.1 0.4 collective-permute-done.below
  48.4 1.0 %shard_map.45 = f32[8,16,64,128]{3,2,1,0:T(8,128)} custom-call(f32[8,16,64,128]{3,2,1,0:T(8,128)S(1)} %get-tuple-element.8.final, f32[4,64,128]{2,1,0:T(8,128)S(1)} %collective-permute-done.below, f32[8,16,64,128]{3,2,1,0:T(8,128)} %shard_map.44._), custom_call_target="tpu_custom_call", output_to_operand_aliasing={{}: (2, {})} | custom-call | flops 4194304 | bytes 1048576 | tf_op jit(solution)/shard_map/pallas_call | solution.py:549
Async XLA Ops:
  38.5 7.1 %collective-permute-start.2 = (f32[8,64,128]{2,1,0:T(8,128)S(1)}, f32[8,64,128]{2,1,0:T(8,128)S(1)}, u32[]{:S(2)}, u32[]{:S(2)}) collective-permute-start(f32[8,64,128]{2,1,0:T(8,128)S(1)} %get-tuple-element.11), channel_id=1, source_target_pairs={{0,16},{1,17},{2,18},{3,19},{4,20},{5,21},{6,22},{7,23},{8,24},{9,... | collective-permute-start | bytes 786440 | tf_op jit(solution)/shard_map/ppermute | solution.py:478
  39.8 7.2 %collective-permute-start.1 = (f32[4,64,128]{2,1,0:T(8,128)S(1)}, f32[4,64,128]{2,1,0:T(8,128)S(1)}, u32[]{:S(2)}, u32[]{:S(2)}) collective-permute-start(f32[4,64,128]{2,1,0:T(8,128)S(1)} %get-tuple-element.10), channel_id=1, source_target_pairs={{0,16},{1,17},{2,18},{3,19},{4,20},{5,21},{6,22},{7,23},{8,24},{9,... | collective-permute-start | bytes 393224 | tf_op jit(solution)/shard_map/ppermute | solution.py:478
  41.1 7.3 %collective-permute-start = (f32[4,64,128]{2,1,0:T(8,128)S(1)}, f32[4,64,128]{2,1,0:T(8,128)S(1)}, u32[]{:S(2)}, u32[]{:S(2)}) collective-permute-start(f32[4,64,128]{2,1,0:T(8,128)S(1)} %get-tuple-element.9), channel_id=1, source_target_pairs={{0,16},{1,17},{2,18},{3,19},{4,20},{5,21},{6,22},{7,23},{8,24},{9,... | collective-permute-start | bytes 393224 | tf_op jit(solution)/shard_map/ppermute | solution.py:478

commit v2 on v1

--- a/solution.py
+++ b/solution.py
@@ -26,8 +26,8 @@
     return ((0, I // 2), (I // 2, I // 4), (I - I // 4, I // 4))
 
 
-def cut(I, eighths):
-    lead = I * eighths // 8 if I % 8 == 0 else I - I // 2
+def cut(I, sixteenths):
+    lead = I * sixteenths // 16 if I % 16 == 0 else I - I // 2
     return ((0, lead), (lead, I - lead))
 
 
@@ -48,7 +48,7 @@
     ) = refs
     J, I, K, L = field.shape
     grids = (grid0, grid1, grid2)
-    x_parts = [((0, I),)] * (STEPS - 2) + [cut(I, 6), cut(I, 6)]
+    x_parts = [((0, I),)] * (STEPS - 2) + [cut(I, 12), cut(I, 11)]
     x_slot = [step + max(step - STEPS + 2, 0) for step in range(STEPS)]
     U = pieces_of(I, (4, 2))
     inside = pl.ds(PAD, K)
@@ -75,16 +75,17 @@
 
     load_field = [
         pltpu.make_async_copy(
-            field.at[: J - 1], grid0.at[1:J, 1 : I + 1, inside], load.at[0]
-        ),
+            field.at[j], grid0.at[(j + 1) % J, 1 : I + 1, inside], load.at[n]
+        )
+        for n, j in ((0, 0), (1, J - 1))
+    ] + [
         pltpu.make_async_copy(
-            field.at[J - 1], grid0.at[0, 1 : I + 1, inside], load.at[1]
-        ),
+            field.at[1 : J - 1], grid0.at[2:J, 1 : I + 1, inside], load.at[2]
+        )
     ]
-    load_cells = pltpu.make_async_copy(crowd, cells, load.at[2])
+    load_cells = pltpu.make_async_copy(crowd, cells, load.at[3])
     for one in load_field:
         one.start()
-    load_cells.start()
 
     barrier = pltpu.get_barrier_semaphore()
     peers = jnp.int32(1 if paired else 0)
@@ -107,7 +108,7 @@
         at, count = x_parts[step][n]
         columns = pl.ds(at, count)
         if step == 0:
-            source = field.at[out_plane[way], columns]
+            source = grid0.at[out_at[way], pl.ds(1 + at, count), inside]
         else:
             source = part.at[step - 1, way, columns]
         return pltpu.make_async_remote_copy(
@@ -308,8 +309,11 @@
             count = len(x_parts[step])
             start("rows", way, [x_copy(step, way, n) for n in range(count)[low:high]])
 
+    for one in load_field[:2]:
+        one.wait()
     send_plane(0)
     send_columns(0, (0, 1))
+    load_cells.start()
 
     zero = jnp.zeros((K, L), jnp.float32)
     for way in (0, 1):
@@ -333,8 +337,7 @@
 
             loop(0, J, body)
 
-    for one in load_field:
-        one.wait()
+    load_field[2].wait()
     loop(0, J, functools.partial(keep_rims, 0))
     send_rims(0, (0, 1))
     load_cells.wait()
@@ -518,7 +521,7 @@
                 dma((STEPS, 2, 2)),
                 dma((2, 2)),
                 dma((STEPS, 2, 2)),
-                dma((3,)),
+                dma((4,)),
                 pltpu.SemaphoreType.REGULAR,
             ],
             compiler_params=pltpu.CompilerParams(

time: 49.6 us -> 49.4 us (level)
  Pallas kernels: 43.4 us -> 42.8 us
    pallas_call x1, Pallas kernels: 37.9 us -> 37.3 us  [on_device(): pl.pallas_call(functools.partial(march_kernel, sizes), out_shape=(pltpu.V...]
where the time goes in v2:
time: 49.4 us; the launch traced here: 49.2 us
  Pallas kernels  42.8 us (87%)
  starting transfers between devices  3.88 us (8%)
  waiting for transfers between devices  1.81 us (4%)
  between operations  0.69 us (1%)
    pallas_call x1, Pallas kernels, on_device(): pl.pallas_call(functools.partial(march_kernel, sizes), out_shape=(pltpu.V...  37.3 us
    ppermute x3, starting transfers between devices, totals_below(): below = lax.ppermute(total, 'rows', [(r, r + 1) for r in range(n - 1)])  3.88 us
    pallas_call x3, Pallas kernels, on_device(): pl.pallas_call(functools.partial(sum_kernel, scale, at), out_shape=block,...  3.44 us
    pallas_call x1, Pallas kernels, on_device(): pl.pallas_call(functools.partial(end_kernel, scale), out_shape=(block, bl...  2.06 us
    ppermute x3, waiting for transfers between devices, totals_below(): below = lax.ppermute(total, 'rows', [(r, r + 1) for r in range(n - 1)])  1.81 us
  transfers between devices with their start and end apart: 3, of which 2 were waited for; matrix products, arithmetic and copies ran while one was open for 0% of the time, Pallas kernels for 9%

profile of v2, /device:TPU:3, one launch (start us, length us, event | category | flops | bytes accessed | tf_op | source)
XLA Modules:
  0.0 49.2 jit_solution(10615108219204817220)
XLA Ops:
  0.6 37.3 %shard_map.41 = (f32[8,16,64,128]{3,2,1,0:T(8,128)S(1)}, f32[8,64,128]{2,1,0:T(8,128)S(1)}, f32[4,64,128]{2,1,0:T(8,128)S(1)}, f32[4,64,128]{2,1,0:T(8,128)S(1)}) custom-call(f32[8,16,64,128]{3,2,1,0:T(8,128)} %field.1, f32[8,16,64,128]{3,2,1,0:T(8,128)} %crowd.1), custom_call_target="tpu_custom_call" | custom-call | tf_op jit(solution)/shard_map/pallas_call | solution.py:503
  37.9 1.3 %collective-permute-start.2 = (f32[8,64,128]{2,1,0:T(8,128)S(1)}, f32[8,64,128]{2,1,0:T(8,128)S(1)}, u32[]{:S(2)}, u32[]{:S(2)}) collective-permute-start(f32[8,64,128]{2,1,0:T(8,128)S(1)} %get-tuple-element.11), channel_id=1, source_target_pairs={{0,16},{1,17},{2,18},{3,19},{4,20},{5,21},{6,22},{7,23},{8,24},{9,... | collective-permute-start | bytes 786440 | tf_op jit(solution)/shard_map/ppermute | solution.py:481
  39.2 1.3 %collective-permute-start.1 = (f32[4,64,128]{2,1,0:T(8,128)S(1)}, f32[4,64,128]{2,1,0:T(8,128)S(1)}, u32[]{:S(2)}, u32[]{:S(2)}) collective-permute-start(f32[4,64,128]{2,1,0:T(8,128)S(1)} %get-tuple-element.10), channel_id=1, source_target_pairs={{0,16},{1,17},{2,18},{3,19},{4,20},{5,21},{6,22},{7,23},{8,24},{9,... | collective-permute-start | bytes 393224 | tf_op jit(solution)/shard_map/ppermute | solution.py:481
  40.5 1.3 %collective-permute-start = (f32[4,64,128]{2,1,0:T(8,128)S(1)}, f32[4,64,128]{2,1,0:T(8,128)S(1)}, u32[]{:S(2)}, u32[]{:S(2)}) collective-permute-start(f32[4,64,128]{2,1,0:T(8,128)S(1)} %get-tuple-element.9), channel_id=1, source_target_pairs={{0,16},{1,17},{2,18},{3,19},{4,20},{5,21},{6,22},{7,23},{8,24},{9,... | collective-permute-start | bytes 393224 | tf_op jit(solution)/shard_map/ppermute | solution.py:481
  41.8 2.1 %shard_map.42 = (f32[8,16,64,128]{3,2,1,0:T(8,128)}, f32[8,16,64,128]{3,2,1,0:T(8,128)}) custom-call(f32[8,16,64,128]{3,2,1,0:T(8,128)S(1)} %get-tuple-element.8.final), custom_call_target="tpu_custom_call" | custom-call | flops 16777216 | bytes 4194304 | tf_op jit(solution)/shard_map/pallas_call | solution.py:540
  43.9 1.5 %collective-permute-done.2.below = f32[8,64,128]{2,1,0:T(8,128)S(1)} collective-permute-done((f32[8,64,128]{2,1,0:T(8,128)S(1)}, f32[8,64,128]{2,1,0:T(8,128)S(1)}, u32[]{:S(2)}, u32[]{:S(2)}) %collective-permute-start.2) | collective-permute-done | bytes 262176 | tf_op jit(solution)/shard_map/ppermute | solution.py:481
  45.4 1.4 %shard_map.43._ = f32[8,16,64,128]{3,2,1,0:T(8,128)} custom-call(f32[8,16,64,128]{3,2,1,0:T(8,128)S(1)} %get-tuple-element.8.final, f32[8,64,128]{2,1,0:T(8,128)S(1)} %collective-permute-done.2.below, f32[8,16,64,128]{3,2,1,0:T(8,128)} %get-tuple-element.12._), custom_call_target="tpu_custom_call", output_to_operand_aliasing={{}: (2, {})} | custom-call | flops 4194304 | bytes 2097152 | tf_op jit(solution)/shard_map/pallas_call | solution.py:552
  46.8 0.0 collective-permute-done.1.below
  46.8 1.0 %shard_map.44._ = f32[8,16,64,128]{3,2,1,0:T(8,128)} custom-call(f32[8,16,64,128]{3,2,1,0:T(8,128)S(1)} %get-tuple-element.8.final, f32[4,64,128]{2,1,0:T(8,128)S(1)} %collective-permute-done.1.below, f32[8,16,64,128]{3,2,1,0:T(8,128)} %shard_map.43._), custom_call_target="tpu_custom_call", output_to_operand_aliasing={{}: (2, {})} | custom-call | flops 4194304 | bytes 1048576 | tf_op jit(solution)/shard_map/pallas_call | solution.py:552
  47.8 0.4 collective-permute-done.below
  48.2 1.0 %shard_map.45 = f32[8,16,64,128]{3,2,1,0:T(8,128)} custom-call(f32[8,16,64,128]{3,2,1,0:T(8,128)S(1)} %get-tuple-element.8.final, f32[4,64,128]{2,1,0:T(8,128)S(1)} %collective-permute-done.below, f32[8,16,64,128]{3,2,1,0:T(8,128)} %shard_map.44._), custom_call_target="tpu_custom_call", output_to_operand_aliasing={{}: (2, {})} | custom-call | flops 4194304 | bytes 1048576 | tf_op jit(solution)/shard_map/pallas_call | solution.py:552
Async XLA Ops:
  37.9 7.4 %collective-permute-start.2 = (f32[8,64,128]{2,1,0:T(8,128)S(1)}, f32[8,64,128]{2,1,0:T(8,128)S(1)}, u32[]{:S(2)}, u32[]{:S(2)}) collective-permute-start(f32[8,64,128]{2,1,0:T(8,128)S(1)} %get-tuple-element.11), channel_id=1, source_target_pairs={{0,16},{1,17},{2,18},{3,19},{4,20},{5,21},{6,22},{7,23},{8,24},{9,... | collective-permute-start | bytes 786440 | tf_op jit(solution)/shard_map/ppermute | solution.py:481
  39.2 7.5 %collective-permute-start.1 = (f32[4,64,128]{2,1,0:T(8,128)S(1)}, f32[4,64,128]{2,1,0:T(8,128)S(1)}, u32[]{:S(2)}, u32[]{:S(2)}) collective-permute-start(f32[4,64,128]{2,1,0:T(8,128)S(1)} %get-tuple-element.10), channel_id=1, source_target_pairs={{0,16},{1,17},{2,18},{3,19},{4,20},{5,21},{6,22},{7,23},{8,24},{9,... | collective-permute-start | bytes 393224 | tf_op jit(solution)/shard_map/ppermute | solution.py:481
  40.5 7.6 %collective-permute-start = (f32[4,64,128]{2,1,0:T(8,128)S(1)}, f32[4,64,128]{2,1,0:T(8,128)S(1)}, u32[]{:S(2)}, u32[]{:S(2)}) collective-permute-start(f32[4,64,128]{2,1,0:T(8,128)S(1)} %get-tuple-element.9), channel_id=1, source_target_pairs={{0,16},{1,17},{2,18},{3,19},{4,20},{5,21},{6,22},{7,23},{8,24},{9,... | collective-permute-start | bytes 393224 | tf_op jit(solution)/shard_map/ppermute | solution.py:481

commit v3 on v2

--- a/solution.py
+++ b/solution.py
@@ -69,6 +69,9 @@
     in_at = (1, 0)
     rows = ((0, 2), (2, J - 2))
 
+    def lane(axis, way):
+        return way if sizes[axis] > 2 else 0
+
     def target(axis, way):
         n = sizes[axis]
         return {axis: lax.rem(place[axis] + (1 if way == 0 else n - 1), n)}
@@ -114,8 +117,8 @@
         return pltpu.make_async_remote_copy(
             src_ref=source,
             dst_ref=x_in.at[step, way, columns],
-            send_sem=x_send.at[x_slot[step] + n, way],
-            recv_sem=x_recv.at[x_slot[step] + n, way],
+            send_sem=x_send.at[x_slot[step] + n, lane("rows", way)],
+            recv_sem=x_recv.at[x_slot[step] + n, lane("rows", way)],
             device_id=target("rows", way),
             device_id_type=MESH,
         )
@@ -132,8 +135,8 @@
         return pltpu.make_async_remote_copy(
             src_ref=source,
             dst_ref=grids[step].at[pl.ds(at, count), halo, inside],
-            send_sem=z_send.at[way, piece],
-            recv_sem=z_recv.at[step, way, piece],
+            send_sem=z_send.at[lane("cols", way), piece],
+            recv_sem=z_recv.at[step, lane("cols", way), piece],
             device_id=target("cols", way),
             device_id_type=MESH,
         )
@@ -143,8 +146,8 @@
         return pltpu.make_async_remote_copy(
             src_ref=y_out.at[step, 1 - way, pl.ds(at, count)],
             dst_ref=y_in.at[step, way, pl.ds(at, count)],
-            send_sem=y_send.at[way, piece],
-            recv_sem=y_recv.at[step, way, piece],
+            send_sem=y_send.at[lane("slabs", way), piece],
+            recv_sem=y_recv.at[step, lane("slabs", way), piece],
             device_id=target("slabs", way),
             device_id_type=MESH,
         )
@@ -456,25 +459,26 @@
     whole.wait()
 
 
-def sum_kernel(scale, at, final, below, _, potential, sums, sem):
+def sum_kernel(scale, at, final, below, _, potential, sums, carry, sem):
     J = final.shape[0]
     W = below.shape[0]
 
-    def piece(i):
+    def piece(j):
         return pltpu.make_async_copy(
-            sums.at[:, i], potential.at[:, at + i], sem.at[i]
+            sums.at[j], potential.at[j, at : at + W], sem.at[j]
         )
 
     @pl.when(lax.axis_index("rows") > 0)
     def _():
-        for i in range(W):
-            value = below[i]
-            for j in range(J):
-                value = value + final[j, at + i]
+        for j in range(J):
+            before = below if j == 0 else carry
+            for i in range(W):
+                value = before[i] + final[j, at + i]
+                carry[i] = value
                 sums[j, i] = value * scale
-            piece(i).start()
-        for i in range(W):
-            piece(i).wait()
+            piece(j).start()
+        for j in range(J):
+            piece(j).wait()
 
 
 def totals_below(total, n):
@@ -495,6 +499,7 @@
         J, I, K, L = field_values.shape
         widths = [width for _, width in segments_of(I)]
         N = len(widths)
+        lanes = {axis: 2 if sizes[axis] > 2 else 1 for axis in AXES}
         padded = pltpu.VMEM((J, I + 2, K + 2 * PAD, L), jnp.float32)
         block = jax.ShapeDtypeStruct((J, I, K, L), jnp.float32)
         vector = pl.BlockSpec(memory_space=pltpu.VMEM)
@@ -515,12 +520,12 @@
                 pltpu.VMEM((STEPS - 1, 2, I, K, L), jnp.float32),
                 pltpu.VMEM((STEPS, 2, J, I, L), jnp.float32),
                 pltpu.VMEM((STEPS, 2, J, I, L), jnp.float32),
-                dma((STEPS + 2, 2)),
-                dma((STEPS + 2, 2)),
-                dma((2, 2)),
-                dma((STEPS, 2, 2)),
-                dma((2, 2)),
-                dma((STEPS, 2, 2)),
+                dma((STEPS + 2, lanes["rows"])),
+                dma((STEPS + 2, lanes["rows"])),
+                dma((lanes["cols"], 2)),
+                dma((STEPS, lanes["cols"], 2)),
+                dma((lanes["slabs"], 2)),
+                dma((STEPS, lanes["slabs"], 2)),
                 dma((4,)),
                 pltpu.SemaphoreType.REGULAR,
             ],
@@ -556,7 +561,8 @@
                 out_specs=anywhere,
                 scratch_shapes=[
                     pltpu.VMEM((J, width, K, L), jnp.float32),
-                    dma((width,)),
+                    pltpu.VMEM((width, K, L), jnp.float32),
+                    dma((J,)),
                 ],
                 input_output_aliases={2: 0},
                 compiler_params=pltpu.CompilerParams(vmem_limit_bytes=5 * 1024 * 1024),

time: 49.4 us -> 49.4 us (level)
  no operation moved by 1% of the time
where the time goes in v3:
time: 49.4 us; the launch traced here: 49.2 us
  Pallas kernels  42.9 us (87%)
  starting transfers between devices  3.88 us (8%)
  waiting for transfers between devices  1.75 us (4%)
  between operations  0.69 us (1%)
    pallas_call x1, Pallas kernels, on_device(): pl.pallas_call(functools.partial(march_kernel, sizes), out_shape=(pltpu.V...  37.3 us
    ppermute x3, starting transfers between devices, totals_below(): below = lax.ppermute(total, 'rows', [(r, r + 1) for r in range(n - 1)])  3.88 us
    pallas_call x3, Pallas kernels, on_device(): pl.pallas_call(functools.partial(sum_kernel, scale, at), out_shape=block,...  3.53 us
    pallas_call x1, Pallas kernels, on_device(): pl.pallas_call(functools.partial(end_kernel, scale), out_shape=(block, bl...  2.06 us
    ppermute x3, waiting for transfers between devices, totals_below(): below = lax.ppermute(total, 'rows', [(r, r + 1) for r in range(n - 1)])  1.75 us
  transfers between devices with their start and end apart: 3, of which 2 were waited for; matrix products, arithmetic and copies ran while one was open for 0% of the time, Pallas kernels for 9%

profile of v3, /device:TPU:3, one launch (start us, length us, event | category | flops | bytes accessed | tf_op | source)
XLA Modules:
  0.0 49.2 jit_solution(9469189265308700781)
XLA Ops:
  0.6 37.3 %shard_map.41 = (f32[8,16,64,128]{3,2,1,0:T(8,128)S(1)}, f32[8,64,128]{2,1,0:T(8,128)S(1)}, f32[4,64,128]{2,1,0:T(8,128)S(1)}, f32[4,64,128]{2,1,0:T(8,128)S(1)}) custom-call(f32[8,16,64,128]{3,2,1,0:T(8,128)} %field.1, f32[8,16,64,128]{3,2,1,0:T(8,128)} %crowd.1), custom_call_target="tpu_custom_call" | custom-call | tf_op jit(solution)/shard_map/pallas_call | solution.py:508
  37.9 1.3 %collective-permute-start.2 = (f32[8,64,128]{2,1,0:T(8,128)S(1)}, f32[8,64,128]{2,1,0:T(8,128)S(1)}, u32[]{:S(2)}, u32[]{:S(2)}) collective-permute-start(f32[8,64,128]{2,1,0:T(8,128)S(1)} %get-tuple-element.11), channel_id=1, source_target_pairs={{0,16},{1,17},{2,18},{3,19},{4,20},{5,21},{6,22},{7,23},{8,24},{9,... | collective-permute-start | bytes 786440 | tf_op jit(solution)/shard_map/ppermute | solution.py:485
  39.2 1.3 %collective-permute-start.1 = (f32[4,64,128]{2,1,0:T(8,128)S(1)}, f32[4,64,128]{2,1,0:T(8,128)S(1)}, u32[]{:S(2)}, u32[]{:S(2)}) collective-permute-start(f32[4,64,128]{2,1,0:T(8,128)S(1)} %get-tuple-element.10), channel_id=1, source_target_pairs={{0,16},{1,17},{2,18},{3,19},{4,20},{5,21},{6,22},{7,23},{8,24},{9,... | collective-permute-start | bytes 393224 | tf_op jit(solution)/shard_map/ppermute | solution.py:485
  40.5 1.3 %collective-permute-start = (f32[4,64,128]{2,1,0:T(8,128)S(1)}, f32[4,64,128]{2,1,0:T(8,128)S(1)}, u32[]{:S(2)}, u32[]{:S(2)}) collective-permute-start(f32[4,64,128]{2,1,0:T(8,128)S(1)} %get-tuple-element.9), channel_id=1, source_target_pairs={{0,16},{1,17},{2,18},{3,19},{4,20},{5,21},{6,22},{7,23},{8,24},{9,... | collective-permute-start | bytes 393224 | tf_op jit(solution)/shard_map/ppermute | solution.py:485
  41.8 2.1 %shard_map.42 = (f32[8,16,64,128]{3,2,1,0:T(8,128)}, f32[8,16,64,128]{3,2,1,0:T(8,128)}) custom-call(f32[8,16,64,128]{3,2,1,0:T(8,128)S(1)} %get-tuple-element.8.final), custom_call_target="tpu_custom_call" | custom-call | flops 16777216 | bytes 4194304 | tf_op jit(solution)/shard_map/pallas_call | solution.py:545
  43.9 1.5 %collective-permute-done.2.below = f32[8,64,128]{2,1,0:T(8,128)S(1)} collective-permute-done((f32[8,64,128]{2,1,0:T(8,128)S(1)}, f32[8,64,128]{2,1,0:T(8,128)S(1)}, u32[]{:S(2)}, u32[]{:S(2)}) %collective-permute-start.2) | collective-permute-done | bytes 262176 | tf_op jit(solution)/shard_map/ppermute | solution.py:485
  45.4 1.4 %shard_map.43._ = f32[8,16,64,128]{3,2,1,0:T(8,128)} custom-call(f32[8,16,64,128]{3,2,1,0:T(8,128)S(1)} %get-tuple-element.8.final, f32[8,64,128]{2,1,0:T(8,128)S(1)} %collective-permute-done.2.below, f32[8,16,64,128]{3,2,1,0:T(8,128)} %get-tuple-element.12._), custom_call_target="tpu_custom_call", output_to_operand_aliasing={{}: (2, {})} | custom-call | flops 4194304 | bytes 2097152 | tf_op jit(solution)/shard_map/pallas_call | solution.py:557
  46.8 0.0 collective-permute-done.1.below
  46.8 1.1 %shard_map.44._ = f32[8,16,64,128]{3,2,1,0:T(8,128)} custom-call(f32[8,16,64,128]{3,2,1,0:T(8,128)S(1)} %get-tuple-element.8.final, f32[4,64,128]{2,1,0:T(8,128)S(1)} %collective-permute-done.1.below, f32[8,16,64,128]{3,2,1,0:T(8,128)} %shard_map.43._), custom_call_target="tpu_custom_call", output_to_operand_aliasing={{}: (2, {})} | custom-call | flops 4194304 | bytes 1048576 | tf_op jit(solution)/shard_map/pallas_call | solution.py:557
  47.9 0.3 collective-permute-done.below
  48.2 1.0 %shard_map.45 = f32[8,16,64,128]{3,2,1,0:T(8,128)} custom-call(f32[8,16,64,128]{3,2,1,0:T(8,128)S(1)} %get-tuple-element.8.final, f32[4,64,128]{2,1,0:T(8,128)S(1)} %collective-permute-done.below, f32[8,16,64,128]{3,2,1,0:T(8,128)} %shard_map.44._), custom_call_target="tpu_custom_call", output_to_operand_aliasing={{}: (2, {})} | custom-call | flops 4194304 | bytes 1048576 | tf_op jit(solution)/shard_map/pallas_call | solution.py:557
Async XLA Ops:
  37.9 7.4 %collective-permute-start.2 = (f32[8,64,128]{2,1,0:T(8,128)S(1)}, f32[8,64,128]{2,1,0:T(8,128)S(1)}, u32[]{:S(2)}, u32[]{:S(2)}) collective-permute-start(f32[8,64,128]{2,1,0:T(8,128)S(1)} %get-tuple-element.11), channel_id=1, source_target_pairs={{0,16},{1,17},{2,18},{3,19},{4,20},{5,21},{6,22},{7,23},{8,24},{9,... | collective-permute-start | bytes 786440 | tf_op jit(solution)/shard_map/ppermute | solution.py:485
  39.2 7.6 %collective-permute-start.1 = (f32[4,64,128]{2,1,0:T(8,128)S(1)}, f32[4,64,128]{2,1,0:T(8,128)S(1)}, u32[]{:S(2)}, u32[]{:S(2)}) collective-permute-start(f32[4,64,128]{2,1,0:T(8,128)S(1)} %get-tuple-element.10), channel_id=1, source_target_pairs={{0,16},{1,17},{2,18},{3,19},{4,20},{5,21},{6,22},{7,23},{8,24},{9,... | collective-permute-start | bytes 393224 | tf_op jit(solution)/shard_map/ppermute | solution.py:485
  40.5 7.6 %collective-permute-start = (f32[4,64,128]{2,1,0:T(8,128)S(1)}, f32[4,64,128]{2,1,0:T(8,128)S(1)}, u32[]{:S(2)}, u32[]{:S(2)}) collective-permute-start(f32[4,64,128]{2,1,0:T(8,128)S(1)} %get-tuple-element.9), channel_id=1, source_target_pairs={{0,16},{1,17},{2,18},{3,19},{4,20},{5,21},{6,22},{7,23},{8,24},{9,... | collective-permute-start | bytes 393224 | tf_op jit(solution)/shard_map/ppermute | solution.py:485

commit v4 on v2

--- a/solution.py
+++ b/solution.py
@@ -84,8 +84,6 @@
         )
     ]
     load_cells = pltpu.make_async_copy(crowd, cells, load.at[3])
-    for one in load_field:
-        one.start()
 
     barrier = pltpu.get_barrier_semaphore()
     peers = jnp.int32(1 if paired else 0)
@@ -102,6 +100,8 @@
                 peers = peers + has_source[axis][way].astype(jnp.int32)
     if paired:
         pl.semaphore_signal(barrier, inc=1, device_id=partner, device_id_type=MESH)
+    for one in load_field:
+        one.start()
     pl.semaphore_wait(barrier, peers)
 
     def x_copy(step, way, n):

time: 49.4 us -> 49.4 us (level)
  no operation moved by 1% of the time
where the time goes in v4:
time: 49.4 us; the launch traced here: 49.2 us
  Pallas kernels  42.8 us (87%)
  starting transfers between devices  3.88 us (8%)
  waiting for transfers between devices  1.81 us (4%)
  between operations  0.69 us (1%)
    pallas_call x1, Pallas kernels, on_device(): pl.pallas_call(functools.partial(march_kernel, sizes), out_shape=(pltpu.V...  37.3 us
    ppermute x3, starting transfers between devices, totals_below(): below = lax.ppermute(total, 'rows', [(r, r + 1) for r in range(n - 1)])  3.88 us
    pallas_call x3, Pallas kernels, on_device(): pl.pallas_call(functools.partial(sum_kernel, scale, at), out_shape=block,...  3.44 us
    pallas_call x1, Pallas kernels, on_device(): pl.pallas_call(functools.partial(end_kernel, scale), out_shape=(block, bl...  2.06 us
    ppermute x3, waiting for transfers between devices, totals_below(): below = lax.ppermute(total, 'rows', [(r, r + 1) for r in range(n - 1)])  1.81 us
  transfers between devices with their start and end apart: 3, of which 2 were waited for; matrix products, arithmetic and copies ran while one was open for 0% of the time, Pallas kernels for 9%

profile of v4, /device:TPU:3, one launch (start us, length us, event | category | flops | bytes accessed | tf_op | source)
XLA Modules:
  0.0 49.2 jit_solution(13972769483455910123)
XLA Ops:
  0.6 37.3 %shard_map.41 = (f32[8,16,64,128]{3,2,1,0:T(8,128)S(1)}, f32[8,64,128]{2,1,0:T(8,128)S(1)}, f32[4,64,128]{2,1,0:T(8,128)S(1)}, f32[4,64,128]{2,1,0:T(8,128)S(1)}) custom-call(f32[8,16,64,128]{3,2,1,0:T(8,128)} %field.1, f32[8,16,64,128]{3,2,1,0:T(8,128)} %crowd.1), custom_call_target="tpu_custom_call" | custom-call | tf_op jit(solution)/shard_map/pallas_call | solution.py:503
  37.9 1.3 %collective-permute-start.2 = (f32[8,64,128]{2,1,0:T(8,128)S(1)}, f32[8,64,128]{2,1,0:T(8,128)S(1)}, u32[]{:S(2)}, u32[]{:S(2)}) collective-permute-start(f32[8,64,128]{2,1,0:T(8,128)S(1)} %get-tuple-element.11), channel_id=1, source_target_pairs={{0,16},{1,17},{2,18},{3,19},{4,20},{5,21},{6,22},{7,23},{8,24},{9,... | collective-permute-start | bytes 786440 | tf_op jit(solution)/shard_map/ppermute | solution.py:481
  39.2 1.3 %collective-permute-start.1 = (f32[4,64,128]{2,1,0:T(8,128)S(1)}, f32[4,64,128]{2,1,0:T(8,128)S(1)}, u32[]{:S(2)}, u32[]{:S(2)}) collective-permute-start(f32[4,64,128]{2,1,0:T(8,128)S(1)} %get-tuple-element.10), channel_id=1, source_target_pairs={{0,16},{1,17},{2,18},{3,19},{4,20},{5,21},{6,22},{7,23},{8,24},{9,... | collective-permute-start | bytes 393224 | tf_op jit(solution)/shard_map/ppermute | solution.py:481
  40.5 1.3 %collective-permute-start = (f32[4,64,128]{2,1,0:T(8,128)S(1)}, f32[4,64,128]{2,1,0:T(8,128)S(1)}, u32[]{:S(2)}, u32[]{:S(2)}) collective-permute-start(f32[4,64,128]{2,1,0:T(8,128)S(1)} %get-tuple-element.9), channel_id=1, source_target_pairs={{0,16},{1,17},{2,18},{3,19},{4,20},{5,21},{6,22},{7,23},{8,24},{9,... | collective-permute-start | bytes 393224 | tf_op jit(solution)/shard_map/ppermute | solution.py:481
  41.8 2.1 %shard_map.42 = (f32[8,16,64,128]{3,2,1,0:T(8,128)}, f32[8,16,64,128]{3,2,1,0:T(8,128)}) custom-call(f32[8,16,64,128]{3,2,1,0:T(8,128)S(1)} %get-tuple-element.8.final), custom_call_target="tpu_custom_call" | custom-call | flops 16777216 | bytes 4194304 | tf_op jit(solution)/shard_map/pallas_call | solution.py:540
  43.9 1.5 %collective-permute-done.2.below = f32[8,64,128]{2,1,0:T(8,128)S(1)} collective-permute-done((f32[8,64,128]{2,1,0:T(8,128)S(1)}, f32[8,64,128]{2,1,0:T(8,128)S(1)}, u32[]{:S(2)}, u32[]{:S(2)}) %collective-permute-start.2) | collective-permute-done | bytes 262176 | tf_op jit(solution)/shard_map/ppermute | solution.py:481
  45.3 1.4 %shard_map.43._ = f32[8,16,64,128]{3,2,1,0:T(8,128)} custom-call(f32[8,16,64,128]{3,2,1,0:T(8,128)S(1)} %get-tuple-element.8.final, f32[8,64,128]{2,1,0:T(8,128)S(1)} %collective-permute-done.2.below, f32[8,16,64,128]{3,2,1,0:T(8,128)} %get-tuple-element.12._), custom_call_target="tpu_custom_call", output_to_operand_aliasing={{}: (2, {})} | custom-call | flops 4194304 | bytes 2097152 | tf_op jit(solution)/shard_map/pallas_call | solution.py:552
  46.7 0.0 collective-permute-done.1.below
  46.8 1.0 %shard_map.44._ = f32[8,16,64,128]{3,2,1,0:T(8,128)} custom-call(f32[8,16,64,128]{3,2,1,0:T(8,128)S(1)} %get-tuple-element.8.final, f32[4,64,128]{2,1,0:T(8,128)S(1)} %collective-permute-done.1.below, f32[8,16,64,128]{3,2,1,0:T(8,128)} %shard_map.43._), custom_call_target="tpu_custom_call", output_to_operand_aliasing={{}: (2, {})} | custom-call | flops 4194304 | bytes 1048576 | tf_op jit(solution)/shard_map/pallas_call | solution.py:552
  47.8 0.4 collective-permute-done.below
  48.2 1.0 %shard_map.45 = f32[8,16,64,128]{3,2,1,0:T(8,128)} custom-call(f32[8,16,64,128]{3,2,1,0:T(8,128)S(1)} %get-tuple-element.8.final, f32[4,64,128]{2,1,0:T(8,128)S(1)} %collective-permute-done.below, f32[8,16,64,128]{3,2,1,0:T(8,128)} %shard_map.44._), custom_call_target="tpu_custom_call", output_to_operand_aliasing={{}: (2, {})} | custom-call | flops 4194304 | bytes 1048576 | tf_op jit(solution)/shard_map/pallas_call | solution.py:552
Async XLA Ops:
  37.9 7.4 %collective-permute-start.2 = (f32[8,64,128]{2,1,0:T(8,128)S(1)}, f32[8,64,128]{2,1,0:T(8,128)S(1)}, u32[]{:S(2)}, u32[]{:S(2)}) collective-permute-start(f32[8,64,128]{2,1,0:T(8,128)S(1)} %get-tuple-element.11), channel_id=1, source_target_pairs={{0,16},{1,17},{2,18},{3,19},{4,20},{5,21},{6,22},{7,23},{8,24},{9,... | collective-permute-start | bytes 786440 | tf_op jit(solution)/shard_map/ppermute | solution.py:481
  39.2 7.5 %collective-permute-start.1 = (f32[4,64,128]{2,1,0:T(8,128)S(1)}, f32[4,64,128]{2,1,0:T(8,128)S(1)}, u32[]{:S(2)}, u32[]{:S(2)}) collective-permute-start(f32[4,64,128]{2,1,0:T(8,128)S(1)} %get-tuple-element.10), channel_id=1, source_target_pairs={{0,16},{1,17},{2,18},{3,19},{4,20},{5,21},{6,22},{7,23},{8,24},{9,... | collective-permute-start | bytes 393224 | tf_op jit(solution)/shard_map/ppermute | solution.py:481
  40.5 7.6 %collective-permute-start = (f32[4,64,128]{2,1,0:T(8,128)S(1)}, f32[4,64,128]{2,1,0:T(8,128)S(1)}, u32[]{:S(2)}, u32[]{:S(2)}) collective-permute-start(f32[4,64,128]{2,1,0:T(8,128)S(1)} %get-tuple-element.9), channel_id=1, source_target_pairs={{0,16},{1,17},{2,18},{3,19},{4,20},{5,21},{6,22},{7,23},{8,24},{9,... | collective-permute-start | bytes 393224 | tf_op jit(solution)/shard_map/ppermute | solution.py:481
